TPU v7x, 32 devices: a whole 2x2x4 slice. The times are simulated.
32 devices in a mesh: grp: 4 (over z), sp: 8 (over y, x, core).
Axes of the slice: x: 2, y: 2, z: 4, core: 2. Of those that a mesh axis runs over, the one named last changes fastest.
Arguments:
- tokens: bfloat16 [2048, 2880], P(('grp', 'sp')), may hold values from -36 to 36
- query_weight: bfloat16 [2880, 2048], P(None, 'sp'), may hold values from -0.109375 to 0.109375
- key_value_weight: bfloat16 [2880, 1024], replicated, may hold values from -0.109375 to 0.109375
- block_places: int32 [16], replicated, may hold values from 0 to 15, each once
- sinks: float32 [32], replicated, may hold values from -1 to 5
Outputs:
- attended: bfloat16 [2048, 2048], P(('grp', 'sp'))
Inputs may be any that keep to these rules, and one draw needn't show every extreme that they name: `block_places`: every sequence block appears once.
All inputs are finite; a program needn't handle non-finite values.
Results may differ from a plain program's by a relative error of at most 0.008.
The roundings to bfloat16 on the way count: a program that leaves them out, or rounds other values in their place, can miss the bound.
Values may be sent and summed in bfloat16 or wider, within the bound.
A program may use at most 128 MiB of HBM per device.

v0:
```python
import jax
import jax.numpy as jnp
from jax import lax
from jax.sharding import PartitionSpec as P

QUERY_HEADS = 32
HEAD_SIZE = 64
BPG = 4
rope_base = 150000.0
neg_large = -1e30


def rotate(vectors, angles):
    middle = vectors.shape[-1] // 2
    first_half = vectors[..., :middle]
    second_half = vectors[..., middle:]
    cosine = jnp.cos(angles)
    sine_part = jnp.sin(angles)
    return jnp.concatenate(
        [
            first_half * cosine - second_half * sine_part,
            second_half * cosine + first_half * sine_part,
        ],
        axis=-1,
    )


def locate(stored, block_rows, block_places):
    blocks = stored // block_rows
    table = jnp.arange(block_places.shape[0], dtype=jnp.int32)
    onehot = (blocks[:, None] == table[None, :]).astype(jnp.int32)
    return jnp.sum(onehot * block_places[None, :], axis=1) * block_rows + stored % block_rows


def prepare(projected, own_places, query_cols, kv_cols, head_count):
    row_count = projected.shape[0]
    inverse = rope_base ** (-(jnp.arange(HEAD_SIZE // 2, dtype=jnp.float32) * 2.0) / HEAD_SIZE)
    angles = own_places.astype(jnp.float32)[:, None, None] * inverse[None, None, :]
    queries = rotate(
        projected[:, :query_cols].reshape(row_count, query_cols // HEAD_SIZE, HEAD_SIZE), angles
    ).astype(jnp.bfloat16)
    rotated_keys = rotate(
        projected[:, query_cols : query_cols + kv_cols].reshape(row_count, head_count, HEAD_SIZE),
        angles,
    )
    key_value_pair = jnp.concatenate(
        [rotated_keys.reshape(row_count, kv_cols), projected[:, query_cols + kv_cols :]], axis=1
    ).astype(jnp.bfloat16)
    return (queries, key_value_pair)


def attend(state, queries, query_places, key_value_pair, key_places, head_count):
    maxima, totals, mixture = state
    key_count = key_value_pair.shape[0]
    column_half = key_value_pair.shape[1] // 2
    key_part = key_value_pair[:, :column_half].reshape(key_count, head_count, HEAD_SIZE)
    value_part = key_value_pair[:, column_half:].reshape(key_count, head_count, HEAD_SIZE)
    scores = jnp.einsum(
        "qhgd,khd->hgqk", queries, key_part, preferred_element_type=jnp.float32
    ) * HEAD_SIZE ** (-0.5)
    allowed = key_places[None, :] <= query_places[:, None]
    scores = jnp.where(allowed, scores, neg_large)
    updated = jnp.maximum(maxima, jnp.max(scores, axis=-1))
    weights = jnp.where(allowed, jnp.exp(scores - updated[..., None]), 0.0)
    factor = jnp.exp(maxima - updated)
    totals = totals * factor + jnp.sum(weights, axis=-1)
    mixture = mixture * factor[..., None] + jnp.einsum(
        "hgqk,khd->hgqd",
        weights.astype(jnp.bfloat16),
        value_part,
        preferred_element_type=jnp.float32,
    )
    return (updated, totals, mixture)


def per_device(tokens, query_weight, key_value_weight, block_places, sinks):
    sp_count = lax.axis_size("sp")
    local_rows = tokens.shape[0]
    group_rows = local_rows * sp_count
    block_rows = group_rows // BPG
    kv_total = key_value_weight.shape[1] // (2 * HEAD_SIZE)
    sp_place = lax.axis_index("sp")
    grp_place = lax.axis_index("grp")
    query_cols = query_weight.shape[1]
    query_heads = query_cols // HEAD_SIZE
    head_count = max(kv_total // sp_count, 1)
    kv_cols = head_count * HEAD_SIZE
    first_head = sp_place * query_heads // (QUERY_HEADS // kv_total)
    key_weight = lax.dynamic_slice_in_dim(key_value_weight, first_head * HEAD_SIZE, kv_cols, 1)
    value_weight = lax.dynamic_slice_in_dim(
        key_value_weight, kv_total * HEAD_SIZE + first_head * HEAD_SIZE, kv_cols, 1
    )
    joined = jnp.concatenate([query_weight, key_weight, value_weight], axis=1)
    projected = jnp.dot(
        lax.all_gather(tokens, "sp", axis=0, tiled=True), joined, preferred_element_type=jnp.float32
    )
    query_local = jnp.arange(group_rows, dtype=jnp.int32)
    head_first = sp_place * query_heads
    own_places = locate(grp_place * group_rows + query_local, block_rows, block_places)
    queries, key_value_pair = prepare(projected, own_places, query_cols, kv_cols, head_count)
    query_sharing = query_heads // head_count
    head_sinks = lax.dynamic_slice_in_dim(sinks, head_first, query_heads, 0).reshape(
        head_count, query_sharing
    )
    sink_rows = jnp.broadcast_to(head_sinks[:, :, None], (head_count, query_sharing, group_rows))
    query_block4 = queries.reshape(group_rows, head_count, query_sharing, HEAD_SIZE)
    initial = (
        sink_rows,
        jnp.ones((head_count, query_sharing, group_rows), jnp.float32),
        jnp.zeros((head_count, query_sharing, group_rows, HEAD_SIZE), jnp.float32),
    )
    piece = lax.all_gather(key_value_pair, "grp", axis=0, tiled=True)
    step_rows = min(piece.shape[0], group_rows)
    turns = piece.shape[0] // step_rows

    def visit(turn, inner):
        offset = turn * step_rows
        piece_rows = lax.dynamic_slice_in_dim(piece, offset, step_rows, 0)
        position = offset + jnp.arange(step_rows, dtype=jnp.int32)
        stored = position // group_rows * group_rows + position % group_rows
        key_places = locate(stored, block_rows, block_places)
        return attend(inner, query_block4, own_places, piece_rows, key_places, head_count)

    maxima, totals, mixture = lax.fori_loop(0, turns, visit, initial)
    normed = jnp.transpose(mixture, (2, 0, 1, 3)) / jnp.transpose(totals, (2, 0, 1))[..., None]
    attended = normed.reshape(group_rows, query_cols).astype(jnp.bfloat16)
    return lax.all_to_all(attended, "sp", split_axis=0, concat_axis=1, tiled=True)


def solution(mesh):
    in_specs = (P(("grp", "sp"), None), P(None, "sp"), P(), P(), P())
    out_specs = P(("grp", "sp"), None)
    return jax.shard_map(
        per_device, mesh=mesh, in_specs=in_specs, out_specs=out_specs, check_vma=False
    )
```

profile of v0, /device:TPU:0, one launch (start us, length us, event | category | flops | bytes accessed | tf_op | source)
XLA Modules:
  0.0 114.0 jit_solution(16821734951300925589)
XLA Ops:
  6.5 0.0 all-gather.2.cloned.1.call-start
  6.5 0.7 all-gather.2.cloned.1.call-update
  7.3 0.7 dynamic_slice.20
  8.1 0.7 select_reduce_fusion.1
  8.8 0.3 multiply_cosine_fusion
  9.1 1.8 %constant_dynamic-slice_fusion.1 = (bf16[2880,64]{1,0:T(8,128)(2,1)S(1)}, bf16[2880,64]{1,0:T(8,128)(2,1)S(1)}) fusion(bf16[2880,1024]{1,0:T(8,128)(2,1)} %param.9, s32[]{:T(128)S(6)} %select_n.163, s32[]{:T(128)S(6)} %select_n.164), kind=kLoop, calls=%fused_computation.92 | loop fusion | bytes 1474568 | tf_op jit(solution)/shard_map/dynamic_slice | solution.py:89
  11.0 32.6 %all-gather.2.cloned.1.call-done = bf16[512,2880]{1,0:T(8,128)(2,1)} async-done(((bf16[64,2880]{1,0:T(8,128)(2,1)}), bf16[512,2880]{1,0:T(8,128)(2,1)}) %all-gather.2.cloned.1.call-update) | async-done | bytes 2949136 | tf_op jit(solution)/shard_map/all_gather | solution.py:95
  43.6 0.0 copy-start.1
  43.6 4.1 %fusion.32 = f32[512,384]{0,1:T(8,128)S(1)} fusion(bf16[512,2880]{1,0:T(8,128)(2,1)} %all-gather.2.cloned.1.call-done, bf16[2880,64]{1,0:T(8,128)(2,1)S(1)} %get-tuple-element.296, bf16[2880,64]{1,0:T(8,128)(2,1)S(1)} %get-tuple-element.295, bf16[2880,256]{1,0:T(8,128)(2,1)} %param.8), kind=kOutput, calls=%fused_computation.53 | convolution fusion | flops 1139097600 | bytes 5947392 | tf_op jit(solution)/shard_map/dot_general | solution.py:94
  47.8 0.3 fusion.43
  48.2 16.0 %all_gather.7 = bf16[2048,128]{0,1:T(8,128)(2,1)S(1)} all-gather(bf16[512,128]{0,1:T(8,128)(2,1)S(1)} %pad_maximum_fusion.1), channel_id=1, replica_groups=mesh['grp'=4,'sp'=8] {'grp'}, dimensions={0}, use_global_device_ids=true | all-gather | bytes 655360 | tf_op jit(solution)/shard_map/all_gather | solution.py:112
  64.2 0.1 fusion.36
  64.3 0.1 broadcast_in_dim.74
  64.4 0.0 copy-done.1
  64.4 31.9 %while.21 = (s32[]{:T(128)}, f32[1,4,512]{2,1,0:T(4,128)S(1)}, f32[1,4,512]{2,1,0:T(4,128)S(1)}, f32[1,4,512,64]{2,3,1,0:T(8,128)S(1)}, s32[16]{0:T(128)S(1)}, /...) while((s32[]{:T(128)}, f32[1,4,512]{2,1,0:T(4,128)S(1)}, ...), condition=%wide.region_5.6_spmd.clone, body=%wide.region_1.5_spmd.clone.sunk | while | flops 282791424 | bytes 31996208 | solution.py:124
  64.4 0.1 select_reduce_fusion.3
  64.5 0.2 broadcast_compare_fusion.3
  64.7 2.8 %fusion.62 = (f32[4,512]{1,0:T(4,128)S(1)}, f32[512,512,4]{1,0,2:T(8,128)}) fusion(pred[512,512]{0,1:T(8,128)(4,1)S(1)} %broadcast_compare_fusion.3, bf16[512,1,4,64]{0,3,2,1:T(8,128)(2,1)S(1)} %get-tuple-element.393, bf16[2048,128]{0,1:T(8,128)(2,1)S(1)} %get-tuple-element.392, s32[]{:T(128)S(6)} %select_n.256), kind=kOutput, calls=%fused_computation.2.clone.1 | convolution fusion | flops 137361408 | bytes 4792324 | tf_op jit(solution)/shard_map/while/body/eval_jaxpr/qhgd,khd->hgqk/dot_general | solution.py:58
  67.5 0.0 copy-start
  67.6 3.7 %fusion.65 = f32[1,4,512,64]{2,3,1,0:T(8,128)S(1)} fusion(f32[512,512,4]{1,0,2:T(8,128)} %get-tuple-element.358, f32[4,512]{1,0:T(4,128)S(1)} %bitcast.99, pred[512,512]{0,1:T(8,128)(4,1)S(1)} %broadcast_compare_fusion.3, f32[1,4,512,64]{2,3,1,0:T(8,128)S(1)} %get-tuple-element.376, f32[4,512]{1,0:T(4,128)S(1)} %get-tuple-element.359, ...), kind=kOutput, calls=%fused_computation.9.clone.1 | convolution fusion | flops 139853824 | bytes 5586953 | tf_op jit(solution)/shard_map/while/body/eval_jaxpr/hgqk,khd->hgqd/dot_general | solution.py:67
  71.3 0.0 copy-done
  71.3 1.0 fusion.64
  72.4 0.1 select_reduce_fusion.3
  72.5 0.2 broadcast_compare_fusion.3
  72.7 2.8 %fusion.62 = (f32[4,512]{1,0:T(4,128)S(1)}, f32[512,512,4]{1,0,2:T(8,128)}) fusion(pred[512,512]{0,1:T(8,128)(4,1)S(1)} %broadcast_compare_fusion.3, bf16[512,1,4,64]{0,3,2,1:T(8,128)(2,1)S(1)} %get-tuple-element.393, bf16[2048,128]{0,1:T(8,128)(2,1)S(1)} %get-tuple-element.392, s32[]{:T(128)S(6)} %select_n.256), kind=kOutput, calls=%fused_computation.2.clone.1 | convolution fusion | flops 137361408 | bytes 4792324 | tf_op jit(solution)/shard_map/while/body/eval_jaxpr/qhgd,khd->hgqk/dot_general | solution.py:58
  75.5 0.0 copy-start
  75.6 3.7 %fusion.65 = f32[1,4,512,64]{2,3,1,0:T(8,128)S(1)} fusion(f32[512,512,4]{1,0,2:T(8,128)} %get-tuple-element.358, f32[4,512]{1,0:T(4,128)S(1)} %bitcast.99, pred[512,512]{0,1:T(8,128)(4,1)S(1)} %broadcast_compare_fusion.3, f32[1,4,512,64]{2,3,1,0:T(8,128)S(1)} %get-tuple-element.376, f32[4,512]{1,0:T(4,128)S(1)} %get-tuple-element.359, ...), kind=kOutput, calls=%fused_computation.9.clone.1 | convolution fusion | flops 139853824 | bytes 5586953 | tf_op jit(solution)/shard_map/while/body/eval_jaxpr/hgqk,khd->hgqd/dot_general | solution.py:67
  79.3 0.0 copy-done
  79.3 1.0 fusion.64
  80.4 0.1 select_reduce_fusion.3
  80.5 0.2 broadcast_compare_fusion.3
  80.7 2.8 %fusion.62 = (f32[4,512]{1,0:T(4,128)S(1)}, f32[512,512,4]{1,0,2:T(8,128)}) fusion(pred[512,512]{0,1:T(8,128)(4,1)S(1)} %broadcast_compare_fusion.3, bf16[512,1,4,64]{0,3,2,1:T(8,128)(2,1)S(1)} %get-tuple-element.393, bf16[2048,128]{0,1:T(8,128)(2,1)S(1)} %get-tuple-element.392, s32[]{:T(128)S(6)} %select_n.256), kind=kOutput, calls=%fused_computation.2.clone.1 | convolution fusion | flops 137361408 | bytes 4792324 | tf_op jit(solution)/shard_map/while/body/eval_jaxpr/qhgd,khd->hgqk/dot_general | solution.py:58
  83.5 0.0 copy-start
  83.5 3.7 %fusion.65 = f32[1,4,512,64]{2,3,1,0:T(8,128)S(1)} fusion(f32[512,512,4]{1,0,2:T(8,128)} %get-tuple-element.358, f32[4,512]{1,0:T(4,128)S(1)} %bitcast.99, pred[512,512]{0,1:T(8,128)(4,1)S(1)} %broadcast_compare_fusion.3, f32[1,4,512,64]{2,3,1,0:T(8,128)S(1)} %get-tuple-element.376, f32[4,512]{1,0:T(4,128)S(1)} %get-tuple-element.359, ...), kind=kOutput, calls=%fused_computation.9.clone.1 | convolution fusion | flops 139853824 | bytes 5586953 | tf_op jit(solution)/shard_map/while/body/eval_jaxpr/hgqk,khd->hgqd/dot_general | solution.py:67
  87.2 0.0 copy-done
  87.3 1.0 fusion.64
  88.4 0.1 select_reduce_fusion.3
  88.5 0.2 broadcast_compare_fusion.3
  88.7 2.8 %fusion.62 = (f32[4,512]{1,0:T(4,128)S(1)}, f32[512,512,4]{1,0,2:T(8,128)}) fusion(pred[512,512]{0,1:T(8,128)(4,1)S(1)} %broadcast_compare_fusion.3, bf16[512,1,4,64]{0,3,2,1:T(8,128)(2,1)S(1)} %get-tuple-element.393, bf16[2048,128]{0,1:T(8,128)(2,1)S(1)} %get-tuple-element.392, s32[]{:T(128)S(6)} %select_n.256), kind=kOutput, calls=%fused_computation.2.clone.1 | convolution fusion | flops 137361408 | bytes 4792324 | tf_op jit(solution)/shard_map/while/body/eval_jaxpr/qhgd,khd->hgqk/dot_general | solution.py:58
  91.5 0.0 copy-start
  91.5 3.7 %fusion.65 = f32[1,4,512,64]{2,3,1,0:T(8,128)S(1)} fusion(f32[512,512,4]{1,0,2:T(8,128)} %get-tuple-element.358, f32[4,512]{1,0:T(4,128)S(1)} %bitcast.99, pred[512,512]{0,1:T(8,128)(4,1)S(1)} %broadcast_compare_fusion.3, f32[1,4,512,64]{2,3,1,0:T(8,128)S(1)} %get-tuple-element.376, f32[4,512]{1,0:T(4,128)S(1)} %get-tuple-element.359, ...), kind=kOutput, calls=%fused_computation.9.clone.1 | convolution fusion | flops 139853824 | bytes 5586953 | tf_op jit(solution)/shard_map/while/body/eval_jaxpr/hgqk,khd->hgqd/dot_general | solution.py:67
  95.2 0.0 copy-done
  95.3 1.0 fusion.64
  96.3 0.1 fusion.35
  96.4 0.3 convert_element_type.40
  96.7 0.3 copy.15
  97.0 9.4 %all_to_all.16 = bf16[8,64,256]{2,1,0:T(8,128)(2,1)S(1)} all-to-all(bf16[8,64,256]{2,1,0:T(8,128)(2,1)S(1)} %copy.15), channel_id=1, replica_groups=mesh['grp'=4,'sp'=8] {'sp'}, dimensions={0} | all-to-all | bytes 524288 | tf_op jit(solution)/shard_map/all_to_all | solution.py:127
  106.5 0.7 copy.18
  (31 shorter events, 0.4 us)
Async XLA Ops:
  6.5 37.1 %all-gather.2.cloned.1.call-start = ((), (), s32[]{:S(2)}) async-start(), calls=%async_computation.1 | async-start | bytes 3391488 | tf_op jit(solution)/shard_map/all_gather | solution.py:95
  43.6 20.8 %copy-start.1 = (s32[16]{0:T(128)S(1)}, s32[16]{0:T(128)}, u32[]{:S(2)}) copy-start(s32[16]{0:T(128)} %param.10) | copy-start | bytes 196
  67.5 3.7 %copy-start = (f32[512,512,4]{1,0,2:T(8,128)S(1)}, f32[512,512,4]{1,0,2:T(8,128)}, u32[]{:S(2)}) copy-start(f32[512,512,4]{1,0,2:T(8,128)} %get-tuple-element.358) | copy-start | bytes 12582916 | tf_op jit(solution)/shard_map/while
  75.5 3.7 %copy-start = (f32[512,512,4]{1,0,2:T(8,128)S(1)}, f32[512,512,4]{1,0,2:T(8,128)}, u32[]{:S(2)}) copy-start(f32[512,512,4]{1,0,2:T(8,128)} %get-tuple-element.358) | copy-start | bytes 12582916 | tf_op jit(solution)/shard_map/while
  83.5 3.7 %copy-start = (f32[512,512,4]{1,0,2:T(8,128)S(1)}, f32[512,512,4]{1,0,2:T(8,128)}, u32[]{:S(2)}) copy-start(f32[512,512,4]{1,0,2:T(8,128)} %get-tuple-element.358) | copy-start | bytes 12582916 | tf_op jit(solution)/shard_map/while
  91.5 3.7 %copy-start = (f32[512,512,4]{1,0,2:T(8,128)S(1)}, f32[512,512,4]{1,0,2:T(8,128)}, u32[]{:S(2)}) copy-start(f32[512,512,4]{1,0,2:T(8,128)} %get-tuple-element.358) | copy-start | bytes 12582916 | tf_op jit(solution)/shard_map/while
Sparse Core Ops, SparseCore 0:
  9.2 34.3 all-gather.1
where the time goes:
time: 114 us
  waiting for transfers between devices  33.3 us (29%)
  matrix products  30.1 us (26%)
  blocking collectives  25.5 us (22%)
  between operations  13.6 us (12%)
  other arithmetic  7.27 us (6%)
  local copies, waits for them, and re-layouts  4.05 us (4%)
    all_gather x1, waiting for transfers between devices, per_device(): lax.all_gather(tokens, 'sp', axis=0, tiled=True)  32.6 us
    all_gather x1, blocking collectives, per_device(): piece = lax.all_gather(key_value_pair, 'grp', axis=0, tiled=True)  16 us
    dot_general x4, matrix products, attend(): jnp.einsum('hgqk,khd->hgqd', weights.astype(jnp.bfloat16), value_part, pr...  14.8 us
    dot_general x4, matrix products, attend(): jnp.einsum('qhgd,khd->hgqk', queries, key_part, preferred_element_type=jn...  11.2 us
    all_to_all x1, blocking collectives, per_device(): lax.all_to_all(attended, 'sp', split_axis=0, concat_axis=1, tiled=True)  9.44 us
    reduce_sum x4, other arithmetic, attend(): totals = totals * factor + jnp.sum(weights, axis=-1)  4.17 us
    dot_general x1, matrix products, per_device(): jnp.dot(lax.all_gather(tokens, 'sp', axis=0, tiled=True), joined, preferr...  4.11 us
  transfers between devices with their start and end apart: 1, of which 1 were waited for; matrix products, arithmetic and copies ran while one was open for 3% of the time, Pallas kernels for 0%

commit v1 on v0

--- a/solution.py
+++ b/solution.py
@@ -74,6 +74,11 @@
 
 
 def per_device(tokens, query_weight, key_value_weight, block_places, sinks):
+
+    def words_play(xs):
+        frame_out = lax.all_to_all(jnp.stack(lax.axis_size("grp") * [xs]), "grp", 0, 0)
+        return jnp.concatenate(frame_out, axis=0)
+
     sp_count = lax.axis_size("sp")
     local_rows = tokens.shape[0]
     group_rows = local_rows * sp_count
@@ -109,7 +114,7 @@
         jnp.ones((head_count, query_sharing, group_rows), jnp.float32),
         jnp.zeros((head_count, query_sharing, group_rows, HEAD_SIZE), jnp.float32),
     )
-    piece = lax.all_gather(key_value_pair, "grp", axis=0, tiled=True)
+    piece = words_play(key_value_pair)
     step_rows = min(piece.shape[0], group_rows)
     turns = piece.shape[0] // step_rows
 

time: 114 us -> 118 us (1.035)
  blocking collectives: 25.5 us -> 9.42 us
  waiting for transfers between devices: 33.3 us -> 48.8 us
  starting transfers between devices: 0.01 us -> 4.6 us
    all_gather x1 -> x0, blocking collectives: 16 us -> none  [per_device(): piece = lax.all_gather(key_value_pair, 'grp', axis=0, tiled=True)]
    all_to_all x0 -> x1, waiting for transfers between devices: none -> 14.3 us  [words_play(): lax.all_to_all(jnp.stack(lax.axis_size('grp') * [xs]), 'grp', 0, 0)]
    all_to_all x0 -> x1, starting transfers between devices: none -> 4.6 us  [words_play(): lax.all_to_all(jnp.stack(lax.axis_size('grp') * [xs]), 'grp', 0, 0)]
  transfers between devices with their start and end apart: 1 -> 2, of which waited for: 1 -> 2; matrix products, arithmetic and copies ran while one was open for 3% -> 3% of each run, Pallas kernels for 0% -> 0%
where the time goes in v1:
time: 118 us
  waiting for transfers between devices  48.8 us (41%)
  matrix products  29.8 us (25%)
  between operations  13.5 us (11%)
  blocking collectives  9.42 us (8%)
  other arithmetic  7.26 us (6%)
  starting transfers between devices  4.6 us (4%)
  local copies, waits for them, and re-layouts  4.49 us (4%)
    all_gather x1, waiting for transfers between devices, per_device(): lax.all_gather(tokens, 'sp', axis=0, tiled=True)  33.7 us
    dot_general x4, matrix products, attend(): jnp.einsum('hgqk,khd->hgqd', weights.astype(jnp.bfloat16), value_part, pr...  14.7 us
    all_to_all x1, waiting for transfers between devices, words_play(): lax.all_to_all(jnp.stack(lax.axis_size('grp') * [xs]), 'grp', 0, 0)  14.3 us
    dot_general x4, matrix products, attend(): jnp.einsum('qhgd,khd->hgqk', queries, key_part, preferred_element_type=jn...  11 us
    all_to_all x1, blocking collectives, per_device(): lax.all_to_all(attended, 'sp', split_axis=0, concat_axis=1, tiled=True)  9.42 us
    all_to_all x1, starting transfers between devices, words_play(): lax.all_to_all(jnp.stack(lax.axis_size('grp') * [xs]), 'grp', 0, 0)  4.6 us
    reduce_sum x4, other arithmetic, attend(): totals = totals * factor + jnp.sum(weights, axis=-1)  4.16 us
    dot_general x1, matrix products, per_device(): jnp.dot(lax.all_gather(tokens, 'sp', axis=0, tiled=True), joined, preferr...  4.11 us
  transfers between devices with their start and end apart: 2, of which 2 were waited for; matrix products, arithmetic and copies ran while one was open for 3% of the time, Pallas kernels for 0%

profile of v1, /device:TPU:0, one launch (start us, length us, event | category | flops | bytes accessed | tf_op | source)
XLA Modules:
  0.0 118.2 jit_solution(6765056020342586539)
XLA Ops:
  6.5 0.0 all-gather.2.cloned.1.call-start
  6.5 0.7 all-gather.2.cloned.1.call-update
  7.3 0.7 select_reduce_fusion.1
  8.1 1.8 %constant_dynamic-slice_fusion.1 = (bf16[2880,64]{1,0:T(8,128)(2,1)S(1)}, bf16[2880,64]{1,0:T(8,128)(2,1)S(1)}) fusion(bf16[2880,1024]{1,0:T(8,128)(2,1)} %param.9, s32[]{:T(128)S(6)} %select_n.163, s32[]{:T(128)S(6)} %select_n.164), kind=kLoop, calls=%fused_computation.92 | loop fusion | bytes 1474568 | tf_op jit(solution)/shard_map/dynamic_slice | solution.py:94
  9.9 33.7 %all-gather.2.cloned.1.call-done = bf16[512,2880]{1,0:T(8,128)(2,1)} async-done(((bf16[64,2880]{1,0:T(8,128)(2,1)}), bf16[512,2880]{1,0:T(8,128)(2,1)}) %all-gather.2.cloned.1.call-update) | async-done | bytes 2949136 | tf_op jit(solution)/shard_map/all_gather | solution.py:100
  43.6 4.1 %fusion.32 = f32[512,384]{0,1:T(8,128)S(1)} fusion(bf16[512,2880]{1,0:T(8,128)(2,1)} %all-gather.2.cloned.1.call-done, bf16[2880,64]{1,0:T(8,128)(2,1)S(1)} %get-tuple-element.312, bf16[2880,64]{1,0:T(8,128)(2,1)S(1)} %get-tuple-element.311, bf16[2880,256]{1,0:T(8,128)(2,1)} %param.8), kind=kOutput, calls=%fused_computation.53 | convolution fusion | flops 1139097600 | bytes 5947392 | tf_op jit(solution)/shard_map/dot_general | solution.py:99
  47.7 0.0 copy-start.1
  47.8 0.3 fusion.43
  48.1 0.8 stack.2
  49.0 4.6 %all-to-all-start = ((bf16[4,512,128]{1,2,0:T(8,128)(2,1)}), bf16[4,512,128]{1,2,0:T(8,128)(2,1)S(1)}, u32[]{:S(2)}, u32[]{:S(2)}) async-start(bf16[4,512,128]{1,2,0:T(8,128)(2,1)} %stack.2), calls=%async_computation | async-start | bytes 1048576 | tf_op jit(solution)/shard_map/all_to_all | solution.py:79
  53.6 0.0 copy-done.2
  53.6 0.1 dynamic_slice.20
  53.6 0.3 multiply_cosine_fusion
  54.0 0.1 fusion.36
  54.1 14.3 %all-to-all-done = bf16[4,512,128]{1,2,0:T(8,128)(2,1)S(1)} async-done(((bf16[4,512,128]{1,2,0:T(8,128)(2,1)}), bf16[4,512,128]{1,2,0:T(8,128)(2,1)S(1)}, u32[]{:S(2)}, u32[]{:S(2)}) %all-to-all-start) | async-done | bytes 524320 | tf_op jit(solution)/shard_map/all_to_all | solution.py:79
  68.5 0.3 copy.20
  68.7 0.1 broadcast_in_dim.74
  68.8 0.0 copy-done.1
  68.8 31.7 %while.21 = (s32[]{:T(128)}, f32[1,4,512]{2,1,0:T(4,128)S(1)}, f32[1,4,512]{2,1,0:T(4,128)S(1)}, f32[1,4,512,64]{2,3,1,0:T(8,128)S(1)}, s32[16]{0:T(128)S(1)}, /...) while((s32[]{:T(128)}, f32[1,4,512]{2,1,0:T(4,128)S(1)}, ...), condition=%wide.region_5.6_spmd.clone, body=%wide.region_1.5_spmd.clone.sunk | while | flops 282791424 | bytes 32127280 | solution.py:129
  68.8 0.1 select_reduce_fusion.3
  69.0 0.2 broadcast_compare_fusion.3
  69.2 2.7 %fusion.62 = (f32[4,512]{1,0:T(4,128)S(1)}, f32[512,512,4]{1,0,2:T(8,128)}) fusion(pred[512,512]{0,1:T(8,128)(4,1)S(1)} %broadcast_compare_fusion.3, bf16[512,1,4,64]{0,3,2,1:T(8,128)(2,1)S(1)} %get-tuple-element.409, bf16[2048,128]{1,0:T(8,128)(2,1)S(1)} %get-tuple-element.408, s32[]{:T(128)S(6)} %select_n.256), kind=kOutput, calls=%fused_computation.2.clone.1 | convolution fusion | flops 137361408 | bytes 4857860 | tf_op jit(solution)/shard_map/while/body/eval_jaxpr/qhgd,khd->hgqk/dot_general | solution.py:58
  71.9 0.0 copy-start
  72.0 3.7 %fusion.65 = f32[1,4,512,64]{2,3,1,0:T(8,128)S(1)} fusion(f32[512,512,4]{1,0,2:T(8,128)} %get-tuple-element.374, f32[4,512]{1,0:T(4,128)S(1)} %bitcast.102, pred[512,512]{0,1:T(8,128)(4,1)S(1)} %broadcast_compare_fusion.3, f32[1,4,512,64]{2,3,1,0:T(8,128)S(1)} %get-tuple-element.392, f32[4,512]{1,0:T(4,128)S(1)} %get-tuple-element.375, ...), kind=kOutput, calls=%fused_computation.9.clone.1 | convolution fusion | flops 139853824 | bytes 5652489 | tf_op jit(solution)/shard_map/while/body/eval_jaxpr/hgqk,khd->hgqd/dot_general | solution.py:67
  75.6 0.0 copy-done
  75.6 1.0 fusion.64
  76.8 0.1 select_reduce_fusion.3
  76.9 0.2 broadcast_compare_fusion.3
  77.1 2.7 %fusion.62 = (f32[4,512]{1,0:T(4,128)S(1)}, f32[512,512,4]{1,0,2:T(8,128)}) fusion(pred[512,512]{0,1:T(8,128)(4,1)S(1)} %broadcast_compare_fusion.3, bf16[512,1,4,64]{0,3,2,1:T(8,128)(2,1)S(1)} %get-tuple-element.409, bf16[2048,128]{1,0:T(8,128)(2,1)S(1)} %get-tuple-element.408, s32[]{:T(128)S(6)} %select_n.256), kind=kOutput, calls=%fused_computation.2.clone.1 | convolution fusion | flops 137361408 | bytes 4857860 | tf_op jit(solution)/shard_map/while/body/eval_jaxpr/qhgd,khd->hgqk/dot_general | solution.py:58
  79.9 0.0 copy-start
  79.9 3.7 %fusion.65 = f32[1,4,512,64]{2,3,1,0:T(8,128)S(1)} fusion(f32[512,512,4]{1,0,2:T(8,128)} %get-tuple-element.374, f32[4,512]{1,0:T(4,128)S(1)} %bitcast.102, pred[512,512]{0,1:T(8,128)(4,1)S(1)} %broadcast_compare_fusion.3, f32[1,4,512,64]{2,3,1,0:T(8,128)S(1)} %get-tuple-element.392, f32[4,512]{1,0:T(4,128)S(1)} %get-tuple-element.375, ...), kind=kOutput, calls=%fused_computation.9.clone.1 | convolution fusion | flops 139853824 | bytes 5652489 | tf_op jit(solution)/shard_map/while/body/eval_jaxpr/hgqk,khd->hgqd/dot_general | solution.py:67
  83.6 1.0 fusion.64
  84.7 0.1 select_reduce_fusion.3
  84.8 0.2 broadcast_compare_fusion.3
  85.0 2.7 %fusion.62 = (f32[4,512]{1,0:T(4,128)S(1)}, f32[512,512,4]{1,0,2:T(8,128)}) fusion(pred[512,512]{0,1:T(8,128)(4,1)S(1)} %broadcast_compare_fusion.3, bf16[512,1,4,64]{0,3,2,1:T(8,128)(2,1)S(1)} %get-tuple-element.409, bf16[2048,128]{1,0:T(8,128)(2,1)S(1)} %get-tuple-element.408, s32[]{:T(128)S(6)} %select_n.256), kind=kOutput, calls=%fused_computation.2.clone.1 | convolution fusion | flops 137361408 | bytes 4857860 | tf_op jit(solution)/shard_map/while/body/eval_jaxpr/qhgd,khd->hgqk/dot_general | solution.py:58
  87.8 0.0 copy-start
  87.8 3.7 %fusion.65 = f32[1,4,512,64]{2,3,1,0:T(8,128)S(1)} fusion(f32[512,512,4]{1,0,2:T(8,128)} %get-tuple-element.374, f32[4,512]{1,0:T(4,128)S(1)} %bitcast.102, pred[512,512]{0,1:T(8,128)(4,1)S(1)} %broadcast_compare_fusion.3, f32[1,4,512,64]{2,3,1,0:T(8,128)S(1)} %get-tuple-element.392, f32[4,512]{1,0:T(4,128)S(1)} %get-tuple-element.375, ...), kind=kOutput, calls=%fused_computation.9.clone.1 | convolution fusion | flops 139853824 | bytes 5652489 | tf_op jit(solution)/shard_map/while/body/eval_jaxpr/hgqk,khd->hgqd/dot_general | solution.py:67
  91.5 1.0 fusion.64
  92.6 0.1 select_reduce_fusion.3
  92.7 0.2 broadcast_compare_fusion.3
  93.0 2.7 %fusion.62 = (f32[4,512]{1,0:T(4,128)S(1)}, f32[512,512,4]{1,0,2:T(8,128)}) fusion(pred[512,512]{0,1:T(8,128)(4,1)S(1)} %broadcast_compare_fusion.3, bf16[512,1,4,64]{0,3,2,1:T(8,128)(2,1)S(1)} %get-tuple-element.409, bf16[2048,128]{1,0:T(8,128)(2,1)S(1)} %get-tuple-element.408, s32[]{:T(128)S(6)} %select_n.256), kind=kOutput, calls=%fused_computation.2.clone.1 | convolution fusion | flops 137361408 | bytes 4857860 | tf_op jit(solution)/shard_map/while/body/eval_jaxpr/qhgd,khd->hgqk/dot_general | solution.py:58
  95.7 3.7 %fusion.65 = f32[1,4,512,64]{2,3,1,0:T(8,128)S(1)} fusion(f32[512,512,4]{1,0,2:T(8,128)} %get-tuple-element.374, f32[4,512]{1,0:T(4,128)S(1)} %bitcast.102, pred[512,512]{0,1:T(8,128)(4,1)S(1)} %broadcast_compare_fusion.3, f32[1,4,512,64]{2,3,1,0:T(8,128)S(1)} %get-tuple-element.392, f32[4,512]{1,0:T(4,128)S(1)} %get-tuple-element.375, ...), kind=kOutput, calls=%fused_computation.9.clone.1 | convolution fusion | flops 139853824 | bytes 5652489 | tf_op jit(solution)/shard_map/while/body/eval_jaxpr/hgqk,khd->hgqd/dot_general | solution.py:67
  99.4 1.0 fusion.64
  100.5 0.1 fusion.35
  100.6 0.3 convert_element_type.42
  100.8 0.3 copy.22
  101.2 9.4 %all_to_all.21 = bf16[8,64,256]{2,1,0:T(8,128)(2,1)S(1)} all-to-all(bf16[8,64,256]{2,1,0:T(8,128)(2,1)S(1)} %copy.22), channel_id=1, replica_groups=mesh['grp'=4,'sp'=8] {'sp'}, dimensions={0} | all-to-all | bytes 524288 | tf_op jit(solution)/shard_map/all_to_all | solution.py:132
  110.6 0.7 copy.28
  (36 shorter events, 0.5 us)
Async XLA Ops:
  6.5 37.1 %all-gather.2.cloned.1.call-start = ((), (), s32[]{:S(2)}) async-start(), calls=%async_computation.2 | async-start | bytes 3391488 | tf_op jit(solution)/shard_map/all_gather | solution.py:100
  43.6 10.0 %copy-start.2 = (f32[32]{0:T(128)S(1)}, f32[32]{0:T(128)}, u32[]{:S(2)}) copy-start(f32[32]{0:T(128)} %param.11) | copy-start | bytes 388
  47.7 21.1 %copy-start.1 = (s32[16]{0:T(128)S(1)}, s32[16]{0:T(128)}, u32[]{:S(2)}) copy-start(s32[16]{0:T(128)} %param.10) | copy-start | bytes 196
  49.0 19.5 %all-to-all-start = ((bf16[4,512,128]{1,2,0:T(8,128)(2,1)}), bf16[4,512,128]{1,2,0:T(8,128)(2,1)S(1)}, u32[]{:S(2)}, u32[]{:S(2)}) async-start(bf16[4,512,128]{1,2,0:T(8,128)(2,1)} %stack.2), calls=%async_computation | async-start | bytes 1048576 | tf_op jit(solution)/shard_map/all_to_all | solution.py:79
  71.9 3.7 %copy-start = (f32[512,512,4]{1,0,2:T(8,128)S(1)}, f32[512,512,4]{1,0,2:T(8,128)}, u32[]{:S(2)}) copy-start(f32[512,512,4]{1,0,2:T(8,128)} %get-tuple-element.374) | copy-start | bytes 12582916 | tf_op jit(solution)/shard_map/while
  79.9 3.7 %copy-start = (f32[512,512,4]{1,0,2:T(8,128)S(1)}, f32[512,512,4]{1,0,2:T(8,128)}, u32[]{:S(2)}) copy-start(f32[512,512,4]{1,0,2:T(8,128)} %get-tuple-element.374) | copy-start | bytes 12582916 | tf_op jit(solution)/shard_map/while
  87.8 3.7 %copy-start = (f32[512,512,4]{1,0,2:T(8,128)S(1)}, f32[512,512,4]{1,0,2:T(8,128)}, u32[]{:S(2)}) copy-start(f32[512,512,4]{1,0,2:T(8,128)} %get-tuple-element.374) | copy-start | bytes 12582916 | tf_op jit(solution)/shard_map/while
  95.7 3.7 %copy-start = (f32[512,512,4]{1,0,2:T(8,128)S(1)}, f32[512,512,4]{1,0,2:T(8,128)}, u32[]{:S(2)}) copy-start(f32[512,512,4]{1,0,2:T(8,128)} %get-tuple-element.374) | copy-start | bytes 12582916 | tf_op jit(solution)/shard_map/while
Sparse Core Ops, SparseCore 0:
  9.2 34.3 all-gather.1
